TPU v7x, 32 devices: a whole 2x2x4 slice. The times are simulated.
32 devices in a mesh: fsdp: 8 (over y, x, core), tp: 4 (over z).
Axes of the slice: x: 2, y: 2, z: 4, core: 2. Of those that a mesh axis runs over, the one named last changes fastest.
Arguments:
- partials: bfloat16 [8, 2, 5120, 1024], P('fsdp', None, None, 'tp'), may hold values from -6 to 6
- token_counts: int32 [8], P('fsdp'), may hold values from 100 to 599
- owner_map: int32 [2, 4], replicated, may hold values from 0 to 3, each once within a row
- params: float32 [2, 5120, 1024], P(None, 'fsdp', 'tp'), may hold values from -0.75 to 0.75
- moment1: float32 [2, 5120, 1024], P(None, 'fsdp', 'tp'), may hold values from -0.15625 to 0.15625
- moment2: float32 [2, 5120, 1024], P(None, 'fsdp', 'tp'), may hold values from 0.0001 to 0.004
Outputs:
- new_params: float32 [2, 5120, 1024], P(None, 'fsdp', 'tp')
- new_moment1: float32 [2, 5120, 1024], P(None, 'fsdp', 'tp')
- new_moment2: float32 [2, 5120, 1024], P(None, 'fsdp', 'tp')
- rollout_delta: bfloat16 [2, 5120, 1024], P(None, None, 'tp')
Inputs may be any that keep to these rules, and one draw needn't show every extreme that they name: `owner_map`: each row is a permutation of 0 to 3.
All inputs are finite; a program needn't handle non-finite values.
Results may differ from a plain program's by a relative error of at most 0.0004.
Values may be sent and summed in bfloat16 or wider, within the bound.
A program may use at most 64 MiB of HBM per device.

v0:
```python
import jax
import jax.numpy as jnp
from jax import lax
from jax.sharding import PartitionSpec as P

STEP = 10


def local(partials, token_counts, owner_map, params, moment1, moment2):
    weight = token_counts.astype(jnp.float32)[0]
    total = lax.psum(weight, "fsdp")
    summed = lax.psum_scatter(
        weight * partials[0].astype(jnp.float32), "fsdp", scatter_dimension=1, tiled=True
    )
    grad = summed / total
    first = 0.9 * moment1 + 0.1 * grad
    second = 0.999 * moment2 + 0.001 * grad * grad
    bias_one = 1.0 - 0.9**STEP
    bias_two = 1.0 - 0.999**STEP
    direction = first / bias_one / (jnp.sqrt(second / bias_two) + 1e-08)
    new_params = params - 0.001 * (direction + 0.1 * params)
    delta = direction.astype(jnp.bfloat16)
    owners = lax.axis_size("tp")
    column = lax.axis_index("tp")
    served = lax.dynamic_index_in_dim(owner_map, column, 1, keepdims=False)
    select = served[:, None] == jnp.arange(owners, dtype=jnp.int32)[None, :]
    wide = lax.all_gather(delta, "tp", axis=2, tiled=True)
    block = wide.shape[2] // owners
    split = wide.reshape(wide.shape[0], wide.shape[1], owners, block)
    kept = jnp.where(select[:, None, :, None], split, jnp.zeros((), jnp.bfloat16))
    rollout = lax.all_gather(jnp.sum(kept, axis=2), "fsdp", axis=1, tiled=True)
    return (new_params, first, second, rollout)


def solution(mesh):
    in_specs = (
        P("fsdp", None, None, "tp"),
        P("fsdp"),
        P(),
        P(None, "fsdp", "tp"),
        P(None, "fsdp", "tp"),
        P(None, "fsdp", "tp"),
    )
    out_specs = (
        P(None, "fsdp", "tp"),
        P(None, "fsdp", "tp"),
        P(None, "fsdp", "tp"),
        P(None, None, "tp"),
    )
    return jax.shard_map(local, mesh=mesh, in_specs=in_specs, out_specs=out_specs, check_vma=False)
```

profile of v0, /device:TPU:0, one launch (start us, length us, event | category | flops | bytes accessed | tf_op | source)
XLA Modules:
  0.0 218.2 jit_solution(1838957992258267860)
XLA Ops:
  7.2 0.0 copy-start
  7.2 0.0 reduce-scatter.2.cloned.1.call-start
  7.9 7.3 %multiply_bitcast_fusion = f32[2,5120,256]{2,1,0:T(8,128)} fusion(bf16[1,2,5120,256]{3,2,1,0:T(8,128)(2,1)} %param.6, f32[]{:T(128)} %bitcast), kind=kLoop, calls=%fused_computation | loop fusion | flops 5242880 | bytes 15728644 | tf_op jit(solution)/shard_map/mul | solution.py:13
  15.2 0.0 copy-start.1
  15.2 0.0 copy-start.2
  15.2 0.0 reduce-scatter.2.cloned.1.call-update
  15.2 0.0 all-gather.3.cloned.1.call-start
  15.3 16.3 %psum.7 = f32[]{:T(128)} all-reduce(f32[]{:T(128)} %bitcast), channel_id=1, replica_groups=mesh['fsdp'=8,'tp'=4] {'fsdp'}, use_global_device_ids=true, to_apply=%region_1.0 | all-reduce | flops 1 | bytes 8 | tf_op jit(solution)/shard_map/psum | solution.py:11
  31.6 68.4 %reduce-scatter.2.cloned.1.call-done = f32[2,640,256]{2,1,0:T(8,128)} async-done(((f32[2,5120,256]{2,1,0:T(8,128)}), f32[2,640,256]{2,1,0:T(8,128)}) %reduce-scatter.2.cloned.1.call-update) | async-done | bytes 1310736 | tf_op jit(solution)/shard_map/reduce_scatter | solution.py:12
  100.0 0.0 copy-done.1
  100.0 0.0 copy-done.2
  100.0 4.3 %fusion.1 = (bf16[2,640,256]{2,1,0:T(8,128)(2,1)}, f32[2,640,256]{2,1,0:T(8,128)}, f32[2,640,256]{2,1,0:T(8,128)}) fusion(f32[2,640,256]{2,1,0:T(8,128)} %reduce-scatter.2.cloned.1.call-done, f32[]{:T(128)} %psum.7, f32[2,640,256]{2,1,0:T(8,128)S(1)} %copy-done.1, f32[2,640,256]{2,1,0:T(8,128)S(1)} %copy-done.2), kind=kLoop, calls=%fused_computation.10 | loop fusion | flops 4259840 | bytes 7208964 | tf_op jit(solution)/shard_map/convert_element_type | solution.py:22
  104.3 0.0 all-gather.3.cloned.1.call-update
  104.3 0.0 all-gather.5.cloned.1.call-start
  104.4 0.0 copy-done
  104.4 0.2 dynamic-slice_reduce_fusion
  104.6 0.1 iota_compare_fusion
  104.6 54.7 %all-gather.3.cloned.1.call-done = bf16[2,640,1024]{2,1,0:T(8,128)(2,1)} async-done(((bf16[2,640,256]{2,1,0:T(8,128)(2,1)}), bf16[2,640,1024]{2,1,0:T(8,128)(2,1)}) %all-gather.3.cloned.1.call-update) | async-done | bytes 2621456 | tf_op jit(solution)/shard_map/all_gather | solution.py:27
  159.3 4.3 %reshape.35 = bf16[2,640,4,256]{3,2,1,0:T(4,128)(2,1)S(1)} reshape(bf16[2,640,1024]{2,1,0:T(8,128)(2,1)} %all-gather.3.cloned.1.call-done) | data formatting | bytes 5242880 | tf_op jit(solution)/shard_map/reshape | solution.py:29
  163.6 3.5 %select_reduce_fusion = bf16[2,640,256]{2,1,0:T(8,128)(2,1)} fusion(bf16[2,640,4,256]{3,2,1,0:T(4,128)(2,1)S(1)} %reshape.35, pred[2,4]{1,0:T(4,128)(4,1)S(1)} %iota_compare_fusion), kind=kLoop, calls=%fused_computation.1 | loop fusion | flops 2293760 | bytes 3276808 | tf_op jit(solution)/shard_map/reduce_sum | solution.py:31
  167.2 0.0 all-gather.5.cloned.1.call-update
  167.2 3.8 %multiply_subtract_fusion = f32[2,640,256]{2,1,0:T(8,128)} fusion(f32[2,640,256]{2,1,0:T(8,128)} %param.9, f32[2,640,256]{2,1,0:T(8,128)} %get-tuple-element.13, f32[2,640,256]{2,1,0:T(8,128)} %get-tuple-element.12), kind=kLoop, calls=%fused_computation.4 | loop fusion | flops 2621440 | bytes 5242880 | tf_op jit(solution)/shard_map/sub | solution.py:21
  171.0 35.5 %all-gather.5.cloned.1.call-done = bf16[2,5120,256]{2,1,0:T(8,128)(2,1)} async-done(((bf16[2,640,256]{2,1,0:T(8,128)(2,1)}), bf16[2,5120,256]{2,1,0:T(8,128)(2,1)}) %all-gather.5.cloned.1.call-update) | async-done | bytes 5242896 | tf_op jit(solution)/shard_map/all_gather | solution.py:31
  206.5 5.2 %copy.12 = bf16[2,5120,256]{2,1,0:T(8,128)(2,1)} copy(bf16[2,5120,256]{2,1,0:T(8,128)(2,1)} %all-gather.5.cloned.1.call-done) | data formatting | bytes 10485760
Async XLA Ops:
  7.2 97.2 %copy-start = (s32[2,4]{1,0:T(2,128)S(1)}, s32[2,4]{1,0:T(2,128)}, u32[]{:S(2)}) copy-start(s32[2,4]{1,0:T(2,128)} %param.8) | copy-start | bytes 100
  7.2 92.8 %reduce-scatter.2.cloned.1.call-start = ((), (), s32[]{:S(2)}) async-start(), calls=%async_computation.1 | async-start | bytes 11796480 | tf_op jit(solution)/shard_map/reduce_scatter | solution.py:12
  15.2 84.7 %copy-start.1 = (f32[2,640,256]{2,1,0:T(8,128)S(1)}, f32[2,640,256]{2,1,0:T(8,128)}, u32[]{:S(2)}) copy-start(f32[2,640,256]{2,1,0:T(8,128)} %param.10) | copy-start | bytes 3932164
  15.2 84.7 %copy-start.2 = (f32[2,640,256]{2,1,0:T(8,128)S(1)}, f32[2,640,256]{2,1,0:T(8,128)}, u32[]{:S(2)}) copy-start(f32[2,640,256]{2,1,0:T(8,128)} %param.11) | copy-start | bytes 3932164
  15.2 144.1 %all-gather.3.cloned.1.call-start = ((), (), s32[]{:S(2)}) async-start(), calls=%async_computation.2 | async-start | bytes 3276800 | tf_op jit(solution)/shard_map/all_gather | solution.py:27
  104.3 102.2 %all-gather.5.cloned.1.call-start = ((), (), s32[]{:S(2)}) async-start(), calls=%async_computation.3 | async-start | bytes 5898240 | tf_op jit(solution)/shard_map/all_gather | solution.py:31
Sparse Core Ops, SparseCore 0:
  15.4 84.5 reduce-scatter.1
  104.4 54.8 all-gather.2
  167.3 39.1 all-gather.4
where the time goes:
time: 219 us; the launch traced here: 218 us
  waiting for transfers between devices  159 us (73%)
  other arithmetic  19.1 us (9%)
  blocking collectives  16.3 us (7%)
  between operations  14.4 us (7%)
  local copies, waits for them, and re-layouts  9.72 us (4%)
    reduce_scatter x1, waiting for transfers between devices, local(): lax.psum_scatter(weight * partials[0].astype(jnp.float32), 'fsdp', scatte...  68.4 us
    all_gather x1, waiting for transfers between devices, local(): wide = lax.all_gather(delta, 'tp', axis=2, tiled=True)  54.7 us
    all_gather x1, waiting for transfers between devices, local(): rollout = lax.all_gather(jnp.sum(kept, axis=2), 'fsdp', axis=1, tiled=True)  35.5 us
    psum x1, blocking collectives, local(): total = lax.psum(weight, 'fsdp')  16.3 us
    mul x1, other arithmetic, local(): weight * partials[0].astype(jnp.float32)  7.34 us
    unnamed x7, local copies, waits for them, and re-layouts  5.2 us
  transfers between devices with their start and end apart: 3, of which 3 were waited for; matrix products, arithmetic and copies ran while one was open for 2% of the time, Pallas kernels for 0%

commit v1 on v0

v1 whole, which is shorter than its diff:
```python
import functools

import jax
import jax.numpy as jnp
from jax import lax
from jax.experimental import pallas as pl
from jax.experimental.pallas import tpu as pltpu
from jax.sharding import PartitionSpec as P

STEP = 10
MESH = pl.DeviceIdType.MESH
SPLIT = 4
TILE = 16


def plain(partials, token_counts, owner_map, params, moment1, moment2):
    weight = token_counts.astype(jnp.float32)[0]
    total = lax.psum(weight, "fsdp")
    summed = lax.psum_scatter(
        weight * partials[0].astype(jnp.float32), "fsdp", scatter_dimension=1, tiled=True
    )
    first, second, direction, new_params = adam(summed * (1.0 / total), params, moment1, moment2)
    delta = direction.astype(jnp.bfloat16)
    owners = lax.axis_size("tp")
    served = lax.dynamic_index_in_dim(owner_map, lax.axis_index("tp"), 1, keepdims=False)
    blocks = lax.all_gather(delta, "tp", axis=0)
    kept = jnp.take_along_axis(blocks, served[None, :, None, None], axis=0)[0]
    rollout = lax.all_gather(kept, "fsdp", axis=1, tiled=True)
    return (new_params, first, second, rollout)


def adam(grad, params, moment1, moment2):
    first = 0.9 * moment1 + 0.1 * grad
    second = 0.999 * moment2 + 0.001 * grad * grad
    scale_one = 1.0 / (1.0 - 0.9**STEP)
    scale_two = 1.0 / (1.0 - 0.999**STEP)
    direction = first * scale_one / (jnp.sqrt(second * scale_two) + 1e-08)
    new_params = params - 0.001 * (direction + 0.1 * params)
    return first, second, direction, new_params


def kernel(
    sizes,
    owner_ref,
    w_ref,
    part_ref,
    p_ref,
    m_ref,
    v_ref,
    np_ref,
    nm_ref,
    nv_ref,
    roll_ref,
    wbuf,
    mine,
    theirs,
    acc,
    recv,
    pbuf,
    mbuf,
    vbuf,
    dsend,
    zrecv,
    ag,
    w_s,
    w_r,
    opt_s,
    ld_s,
    raw_s,
    raw_r,
    rs_s,
    rs_r,
    z_s,
    z_r,
    ag_s,
    ag_r,
    fin_s,
    fin_r,
    out_s,
    upd_s,
):
    layers, fsdp, tp, parts, rows = sizes
    chunks = layers * parts
    pairs = fsdp // 2
    bits = pairs.bit_length() - 1
    me = lax.axis_index("fsdp")
    col = lax.axis_index("tp")
    core = lax.rem(me, 2)
    mine_q = me // 2
    partner = mine_q * 2 + (1 - core)

    barrier = pltpu.get_barrier_semaphore()
    for d in range(1, fsdp):
        pl.semaphore_signal(
            barrier, inc=1, device_id={"fsdp": lax.rem(me + d, fsdp)}, device_id_type=MESH
        )
    for d in range(1, tp):
        pl.semaphore_signal(
            barrier, inc=1, device_id={"tp": lax.rem(col + d, tp)}, device_id_type=MESH
        )

    def where(c):
        return c // parts, c % parts

    ends = []
    loads = []
    for c in range(chunks):
        l, k = where(c)
        load = pltpu.make_async_copy(part_ref.at[l, :, core, k], mine.at[c], ld_s.at[c])
        load.start()
        loads.append(load)
    opts = []
    for i, (src, dst) in enumerate(((p_ref, pbuf), (m_ref, mbuf), (v_ref, vbuf))):
        load = pltpu.make_async_copy(src, dst, opt_s.at[i])
        load.start()
        opts.append(load)

    pl.semaphore_wait(barrier, fsdp - 1 + tp - 1)

    def push(src, dst, send, arrive, **device):
        copy = pltpu.make_async_remote_copy(
            src_ref=src,
            dst_ref=dst,
            send_sem=send,
            recv_sem=arrive,
            device_id=device,
            device_id_type=MESH,
        )
        copy.start()
        return copy

    weights = []
    for d in range(1, fsdp):
        weights.append(
            push(w_ref, wbuf.at[d], w_s.at[d], w_r.at[d], fsdp=lax.rem(me + d, fsdp))
        )
    raws = []
    for c in range(chunks):
        l, k = where(c)
        raws.append(
            push(
                part_ref.at[l, :, 1 - core, k],
                theirs.at[c],
                raw_s.at[c],
                raw_r.at[c],
                fsdp=partner,
            )
        )
    for copy in weights:
        copy.wait()
    my_weight = w_ref[0:1, :]
    total = my_weight
    for d in range(1, fsdp):
        total = total + wbuf[d, 0:1, :]
    other_weight = jnp.where(core == 1, wbuf[1, 0:1, :], wbuf[fsdp - 1, 0:1, :])
    scale = 1.0 / total

    def order(c):
        names = list(range(bits))
        return names if c % 2 == 0 else names[::-1]

    def flipped(flips):
        q = mine_q
        for b in flips:
            q = q + (1 - 2 * lax.rem(mine_q // (1 << b), 2)) * (1 << b)
        return q

    step = 2 * TILE if rows % (2 * TILE) == 0 else TILE

    def tiles(body):
        def run(i, carry):
            body(pl.ds(pl.multiple_of(i * step, step), step))
            return carry

        lax.fori_loop(0, rows // step, run, 0)

    halving = {}
    spread = {}
    doubling = {}

    def halve(c, i):
        half = pairs >> (i + 1)
        there = flipped([order(c)[i]]) * 2 + core
        halving[c, i] = push(
            acc.at[c, pl.ds(half, half)],
            recv.at[c, pl.ds(half, half)],
            rs_s.at[c, i],
            rs_r.at[c, i],
            fsdp=there,
        )

    def double(c, j):
        size = 1 << j
        there = flipped([order(c)[j]]) * 2 + core
        doubling[c, j] = push(
            ag.at[c, pl.ds(0, size)],
            ag.at[c, pl.ds(size, size)],
            ag_s.at[c, j],
            ag_r.at[c, j],
            fsdp=there,
        )

    def gather_sum(c):
        loads[c].wait()
        raws[c].wait_recv()
        for pos in range(pairs - 1, -1, -1):
            q = flipped([order(c)[i] for i in range(bits) if pos >> (bits - 1 - i) & 1])

            def body(at):
                acc[c, pos, at, :] = my_weight * mine[c, q, at, :].astype(
                    jnp.float32
                ) + other_weight * theirs[c, q, at, :].astype(jnp.float32)

            tiles(body)
            if pos == pairs // 2:
                halve(c, 0)

    def add(i, c):
        halving[c, i].wait_recv()
        half = pairs >> (i + 1)
        for pos in range(half - 1, -1, -1):

            def body(at):
                acc[c, pos, at, :] = acc[c, pos, at, :] + recv[c, half + pos, at, :]

            tiles(body)
            if pos == half // 2:
                halve(c, i + 1)

    def update(c):
        l, k = where(c)
        halving[c, bits - 1].wait_recv()
        if c == 0:
            for load in opts:
                load.wait()

        def body(at):
            grad = (acc[c, 0, at, :] + recv[c, 1, at, :]) * scale
            first, second, direction, new_params = adam(
                grad, pbuf[l, k, at, :], mbuf[l, k, at, :], vbuf[l, k, at, :]
            )
            dsend[c, at, :] = direction.astype(jnp.bfloat16)
            pbuf[l, k, at, :] = new_params
            mbuf[l, k, at, :] = first
            vbuf[l, k, at, :] = second

        tiles(body)
        for d in range(1, tp):
            spread[c, d] = push(
                dsend.at[c],
                zrecv.at[c, d - 1],
                z_s.at[c, d - 1],
                z_r.at[c, d - 1],
                tp=lax.rem(col + d, tp),
            )
        for i, (src, dst) in enumerate(((pbuf, np_ref), (mbuf, nm_ref), (vbuf, nv_ref))):
            copy = pltpu.make_async_copy(src.at[l, k], dst.at[l, k], upd_s.at[c, i])
            copy.start()
            ends.append(copy.wait)

    def select(c):
        l, k = where(c)
        for d in range(1, tp):
            spread[c, d].wait_recv()
        served = owner_ref[l, col]

        def body(at):
            kept = dsend[c, at, :].astype(jnp.float32)
            for d in range(1, tp):
                kept = jnp.where(
                    served == lax.rem(col + (tp - d), tp),
                    zrecv[c, d - 1, at, :].astype(jnp.float32),
                    kept,
                )
            ag[c, 0, at, :] = kept.astype(jnp.bfloat16)

        tiles(body)
        double(c, 0)

    def finish(c, first, count):
        l, k = where(c)
        for pos in range(first, first + count):
            q = flipped([order(c)[j] for j in range(bits) if pos >> j & 1])
            local = pltpu.make_async_copy(ag.at[c, pos], roll_ref.at[l, q, core, k], out_s.at[c])
            local.start()
            push(
                ag.at[c, pos], roll_ref.at[l, q, core, k], fin_s.at[c], fin_r.at[c], fsdp=partner
            )

    def forward(j, c):
        doubling[c, j].wait_recv()
        if j + 1 < bits:
            double(c, j + 1)
        if j == 0:
            finish(c, 0, 1)
        finish(c, 1 << j, 1 << j)

    stages = [gather_sum]
    stages += [functools.partial(add, i) for i in range(bits - 1)]
    stages += [update, select]
    stages += [functools.partial(forward, j) for j in range(bits)]
    groups = [tuple(range(c, min(c + 2, chunks))) for c in range(0, chunks, 2)]
    for t in range(len(groups) + len(stages) - 1):
        for s, stage in enumerate(stages):
            if 0 <= t - s < len(groups):
                for c in groups[t - s]:
                    stage(c)

    for c in range(chunks):
        raws[c].wait_send()
        for i in range(bits):
            halving[c, i].wait_send()
            doubling[c, i].wait_send()
        for d in range(1, tp):
            spread[c, d].wait_send()
        for sem in (out_s, fin_s, fin_r):
            pltpu.make_async_copy(ag.at[c], ag.at[c], sem.at[c]).wait()
    for wait in ends:
        wait()


def fused(fsdp, tp, partials, token_counts, owner_map, params, moment1, moment2):
    layers, depth, width = partials.shape[1:]
    per = params.shape[1]
    pairs = fsdp // 2
    bits = pairs.bit_length() - 1
    parts = next(n for n in range(SPLIT, 0, -1) if per % (n * TILE) == 0)
    rows = per // parts
    chunks = layers * parts
    weight = jnp.broadcast_to(token_counts.astype(jnp.float32)[:, None], (8, width))
    anywhere = pl.BlockSpec(memory_space=pl.ANY)
    dma = pltpu.SemaphoreType.DMA
    state = (layers, parts, rows, width)
    f32, b16 = jnp.float32, jnp.bfloat16
    outs = pl.pallas_call(
        functools.partial(kernel, (layers, fsdp, tp, parts, rows)),
        out_shape=[
            jax.ShapeDtypeStruct(state, f32),
            jax.ShapeDtypeStruct(state, f32),
            jax.ShapeDtypeStruct(state, f32),
            jax.ShapeDtypeStruct((layers, pairs, 2, parts, rows, width), b16),
        ],
        in_specs=[
            pl.BlockSpec(memory_space=pltpu.SMEM),
            pl.BlockSpec(memory_space=pltpu.VMEM),
            anywhere,
            anywhere,
            anywhere,
            anywhere,
        ],
        out_specs=[anywhere] * 4,
        scratch_shapes=[
            pltpu.VMEM((fsdp, 8, width), f32),
            pltpu.VMEM((chunks, pairs, rows, width), b16),
            pltpu.VMEM((chunks, pairs, rows, width), b16),
            pltpu.VMEM((chunks, pairs, rows, width), f32),
            pltpu.VMEM((chunks, pairs, rows, width), f32),
            pltpu.VMEM(state, f32),
            pltpu.VMEM(state, f32),
            pltpu.VMEM(state, f32),
            pltpu.VMEM((chunks, rows, width), b16),
            pltpu.VMEM((chunks, tp - 1, rows, width), b16),
            pltpu.VMEM((chunks, pairs, rows, width), b16),
            dma((fsdp,)),
            dma((fsdp,)),
            dma((3,)),
            dma((chunks,)),
            dma((chunks,)),
            dma((chunks,)),
            dma((chunks, bits)),
            dma((chunks, bits)),
            dma((chunks, tp - 1)),
            dma((chunks, tp - 1)),
            dma((chunks, bits)),
            dma((chunks, bits)),
            dma((chunks,)),
            dma((chunks,)),
            dma((chunks,)),
            dma((chunks, 3)),
        ],
        compiler_params=pltpu.CompilerParams(
            collective_id=0, has_side_effects=True, vmem_limit_bytes=56 * 1024 * 1024
        ),
    )(
        owner_map,
        weight,
        partials.reshape(layers, pairs, 2, parts, rows, width),
        params.reshape(state),
        moment1.reshape(state),
        moment2.reshape(state),
    )
    return (*(out.reshape(params.shape) for out in outs[:3]), outs[3].reshape(layers, depth, width))


def solution(mesh):
    fsdp, tp = mesh.shape["fsdp"], mesh.shape["tp"]
    local = plain
    if fsdp >= 4 and fsdp & (fsdp - 1) == 0 and tp > 1:
        local = functools.partial(fused, fsdp, tp)
    in_specs = (
        P("fsdp", None, None, "tp"),
        P("fsdp"),
        P(),
        P(None, "fsdp", "tp"),
        P(None, "fsdp", "tp"),
        P(None, "fsdp", "tp"),
    )
    out_specs = (
        P(None, "fsdp", "tp"),
        P(None, "fsdp", "tp"),
        P(None, "fsdp", "tp"),
        P(None, None, "tp"),
    )
    return jax.shard_map(local, mesh=mesh, in_specs=in_specs, out_specs=out_specs, check_vma=False)
```

time: 219 us -> 111 us (0.51)
  waiting for transfers between devices: 159 us -> 0 us
  Pallas kernels: 0 us -> 99.5 us
  other arithmetic: 19.1 us -> 0 us
  blocking collectives: 16.3 us -> 0 us
  between operations: 14.4 us -> 1.3 us
    pallas_call x0 -> x1, Pallas kernels: none -> 99.5 us  [fused(): pl.pallas_call(functools.partial(kernel, (layers, fsdp, tp, parts, rows))...]
    all_gather x2 -> x0, waiting for transfers between devices: 90.1 us -> none  [the longest x1 54.7 us: local(): wide = lax.all_gather(delta, 'tp', axis=2, tiled=True)]
    reduce_scatter x1 -> x0, waiting for transfers between devices: 68.4 us -> none  [local(): lax.psum_scatter(weight * partials[0].astype(jnp.float32), 'fsdp', scatte...]
    psum x1 -> x0, blocking collectives: 16.3 us -> none  [local(): total = lax.psum(weight, 'fsdp')]
    mul x1 -> x0, other arithmetic: 7.34 us -> none  [local(): weight * partials[0].astype(jnp.float32)]
    unnamed x7 -> x6, local copies, waits for them, and re-layouts: 5.2 us -> 9.88 us
    convert_element_type x1 -> x0, other arithmetic: 4.34 us -> none  [local(): delta = direction.astype(jnp.bfloat16)]
    reshape x1 -> x0, local copies, waits for them, and re-layouts: 4.33 us -> none  [local(): split = wide.reshape(wide.shape[0], wide.shape[1], owners, block)]
  transfers between devices with their start and end apart: 3 -> 0, of which waited for: 3 -> 0; matrix products, arithmetic and copies ran while one was open for 2% -> 0% of each run, Pallas kernels for 0% -> 0%
where the time goes in v1:
time: 111 us
  Pallas kernels  99.5 us (90%)
  local copies, waits for them, and re-layouts  10.5 us (9%)
  between operations  1.3 us (1%)
    pallas_call x1, Pallas kernels, fused(): pl.pallas_call(functools.partial(kernel, (layers, fsdp, tp, parts, rows))...  99.5 us
    unnamed x6, local copies, waits for them, and re-layouts  9.88 us

profile of v1, /device:TPU:0, one launch (start us, length us, event | category | flops | bytes accessed | tf_op | source)
XLA Modules:
  0.0 111.3 jit_solution(17480924788236521097)
XLA Ops:
  1.3 0.6 broadcast_in_dim.9.w_ref
  1.9 99.5 %shard_map.93 = (f32[2,4,160,256]{3,2,1,0:T(8,128)}, f32[2,4,160,256]{3,2,1,0:T(8,128)}, f32[2,4,160,256]{3,2,1,0:T(8,128)}, bf16[2,4,2,4,160,256]{5,4,3,2,1,0:T(8,128)(2,1)}) custom-call(s32[2,4]{1,0:T(2,128)} %owner_ref.1, f32[8,256]{1,0:T(8,128)} %broadcast_in_dim.9.w_ref, bf16[2,4,2,4,160,256]{5,4,3,2,1,0:T(8,128)(2,1)} %bitcast.10, ...), custom_call_target="tpu_custom_call" | custom-call | tf_op jit(solution)/shard_map/pallas_call | solution.py:335
  101.4 0.0 copy-start
  101.4 2.6 %copy.15 = f32[2,640,256]{2,1,0:T(8,128)} copy(f32[2,640,256]{2,1,0:T(8,128)} %bitcast.13) | data formatting | bytes 2621440
  104.0 2.5 %copy.16 = f32[2,640,256]{2,1,0:T(8,128)} copy(f32[2,640,256]{2,1,0:T(8,128)} %bitcast.12) | data formatting | bytes 2621440
  106.4 2.5 %copy.17 = f32[2,640,256]{2,1,0:T(8,128)} copy(f32[2,640,256]{2,1,0:T(8,128)} %bitcast.11) | data formatting | bytes 2621440
  108.9 0.0 copy-done
  108.9 2.4 %copy.18 = bf16[2,5120,256]{2,1,0:T(8,128)(2,1)} copy(bf16[2,5120,256]{2,1,0:T(8,128)(2,1)S(1)} %bitcast.9) | data formatting | bytes 10485760
Async XLA Ops:
  101.4 7.5 %copy-start = (bf16[2,4,2,4,160,256]{5,4,3,2,1,0:T(8,128)(2,1)S(1)}, bf16[2,4,2,4,160,256]{5,4,3,2,1,0:T(8,128)(2,1)}, u32[]{:S(2)}) copy-start(bf16[2,4,2,4,160,256]{5,4,3,2,1,0:T(8,128)(2,1)} %get-tuple-element.11) | copy-start | bytes 15728644

commit v2 on v1

--- a/solution.py
+++ b/solution.py
@@ -56,12 +56,8 @@
     theirs,
     acc,
     recv,
-    pbuf,
-    mbuf,
-    vbuf,
-    dsend,
-    zrecv,
-    ag,
+    held,
+    cross,
     w_s,
     w_r,
     opt_s,
@@ -76,8 +72,6 @@
     ag_r,
     fin_s,
     fin_r,
-    out_s,
-    upd_s,
 ):
     layers, fsdp, tp, parts, rows = sizes
     chunks = layers * parts
@@ -89,20 +83,29 @@
     mine_q = me // 2
     partner = mine_q * 2 + (1 - core)
 
+    def away(index, flips):
+        q = index
+        for b in flips:
+            q = q + (1 - 2 * lax.rem(index // (1 << b), 2)) * (1 << b)
+        return q
+
+    def ones(number):
+        return [b for b in range(number.bit_length()) if number >> b & 1]
+
+    tp_bits = tp.bit_length() - 1
     barrier = pltpu.get_barrier_semaphore()
     for d in range(1, fsdp):
         pl.semaphore_signal(
             barrier, inc=1, device_id={"fsdp": lax.rem(me + d, fsdp)}, device_id_type=MESH
         )
-    for d in range(1, tp):
+    for b in range(tp_bits):
         pl.semaphore_signal(
-            barrier, inc=1, device_id={"tp": lax.rem(col + d, tp)}, device_id_type=MESH
+            barrier, inc=1, device_id={"tp": away(col, [b])}, device_id_type=MESH
         )
 
     def where(c):
         return c // parts, c % parts
 
-    ends = []
     loads = []
     for c in range(chunks):
         l, k = where(c)
@@ -110,12 +113,12 @@
         load.start()
         loads.append(load)
     opts = []
-    for i, (src, dst) in enumerate(((p_ref, pbuf), (m_ref, mbuf), (v_ref, vbuf))):
+    for i, (src, dst) in enumerate(((p_ref, np_ref), (m_ref, nm_ref), (v_ref, nv_ref))):
         load = pltpu.make_async_copy(src, dst, opt_s.at[i])
         load.start()
         opts.append(load)
 
-    pl.semaphore_wait(barrier, fsdp - 1 + tp - 1)
+    pl.semaphore_wait(barrier, fsdp - 1 + tp_bits)
 
     def push(src, dst, send, arrive, **device):
         copy = pltpu.make_async_remote_copy(
@@ -160,10 +163,7 @@
         return names if c % 2 == 0 else names[::-1]
 
     def flipped(flips):
-        q = mine_q
-        for b in flips:
-            q = q + (1 - 2 * lax.rem(mine_q // (1 << b), 2)) * (1 << b)
-        return q
+        return away(mine_q, flips)
 
     step = 2 * TILE if rows % (2 * TILE) == 0 else TILE
 
@@ -189,16 +189,20 @@
             fsdp=there,
         )
 
+    def held_rows(c, pos):
+        q = flipped([order(c)[b] for b in ones(pos)])
+        l, k = where(c)
+        return roll_ref.at[l, q, core, k]
+
     def double(c, j):
-        size = 1 << j
         there = flipped([order(c)[j]]) * 2 + core
-        doubling[c, j] = push(
-            ag.at[c, pl.ds(0, size)],
-            ag.at[c, pl.ds(size, size)],
-            ag_s.at[c, j],
-            ag_r.at[c, j],
-            fsdp=there,
-        )
+        for pos in range(1 << j):
+            block = held_rows(c, pos)
+            push(block, block, ag_s.at[c, j], ag_r.at[c, j], fsdp=there)
+
+    def await_blocks(c, count, sem):
+        part = mine.at[c, pl.ds(0, count)]
+        pltpu.make_async_copy(part, part, sem).wait()
 
     def gather_sum(c):
         loads[c].wait()
@@ -237,67 +241,91 @@
         def body(at):
             grad = (acc[c, 0, at, :] + recv[c, 1, at, :]) * scale
             first, second, direction, new_params = adam(
-                grad, pbuf[l, k, at, :], mbuf[l, k, at, :], vbuf[l, k, at, :]
+                grad, np_ref[l, k, at, :], nm_ref[l, k, at, :], nv_ref[l, k, at, :]
             )
-            dsend[c, at, :] = direction.astype(jnp.bfloat16)
-            pbuf[l, k, at, :] = new_params
-            mbuf[l, k, at, :] = first
-            vbuf[l, k, at, :] = second
+            held[c, 0, at, :] = direction.astype(jnp.bfloat16)
+            np_ref[l, k, at, :] = new_params
+            nm_ref[l, k, at, :] = first
+            nv_ref[l, k, at, :] = second
 
         tiles(body)
-        for d in range(1, tp):
-            spread[c, d] = push(
-                dsend.at[c],
-                zrecv.at[c, d - 1],
-                z_s.at[c, d - 1],
-                z_r.at[c, d - 1],
-                tp=lax.rem(col + d, tp),
+        if tp_bits > 1:
+            meet(c, 0)
+        else:
+            hand_over(c)
+
+    def meet(c, b):
+        size = 1 << b
+        spread[c, b] = push(
+            held.at[c, pl.ds(0, size)],
+            held.at[c, pl.ds(size, size)],
+            z_s.at[c, b],
+            z_r.at[c, b],
+            tp=away(col, [b]),
+        )
+
+    def pick(c, at, served, start):
+        kept = start
+        for slot in range(tp // 2):
+            kept = jnp.where(
+                served == away(col, ones(slot)), held[c, slot, at, :].astype(jnp.float32), kept
             )
-        for i, (src, dst) in enumerate(((pbuf, np_ref), (mbuf, nm_ref), (vbuf, nv_ref))):
-            copy = pltpu.make_async_copy(src.at[l, k], dst.at[l, k], upd_s.at[c, i])
-            copy.start()
-            ends.append(copy.wait)
+        return kept.astype(jnp.bfloat16)
+
+    def hand_over(c):
+        l, k = where(c)
+        there = away(col, [tp_bits - 1])
+        served = owner_ref[l, there]
+
+        def body(at):
+            cross[c, 0, at, :] = pick(c, at, served, held[c, 0, at, :].astype(jnp.float32))
+
+        tiles(body)
+        spread[c, tp_bits - 1] = push(
+            cross.at[c, 0],
+            cross.at[c, 1],
+            z_s.at[c, tp_bits - 1],
+            z_r.at[c, tp_bits - 1],
+            tp=there,
+        )
+
+    def met(b, c):
+        spread[c, b].wait_recv()
+        if b + 2 < tp_bits:
+            meet(c, b + 1)
+        else:
+            hand_over(c)
 
     def select(c):
         l, k = where(c)
-        for d in range(1, tp):
-            spread[c, d].wait_recv()
+        spread[c, tp_bits - 1].wait_recv()
         served = owner_ref[l, col]
 
         def body(at):
-            kept = dsend[c, at, :].astype(jnp.float32)
-            for d in range(1, tp):
-                kept = jnp.where(
-                    served == lax.rem(col + (tp - d), tp),
-                    zrecv[c, d - 1, at, :].astype(jnp.float32),
-                    kept,
-                )
-            ag[c, 0, at, :] = kept.astype(jnp.bfloat16)
+            roll_ref[l, mine_q, core, k, at, :] = pick(
+                c, at, served, cross[c, 1, at, :].astype(jnp.float32)
+            )
 
         tiles(body)
         double(c, 0)
+        finish(c, 0, 1)
 
     def finish(c, first, count):
-        l, k = where(c)
         for pos in range(first, first + count):
-            q = flipped([order(c)[j] for j in range(bits) if pos >> j & 1])
-            local = pltpu.make_async_copy(ag.at[c, pos], roll_ref.at[l, q, core, k], out_s.at[c])
-            local.start()
-            push(
-                ag.at[c, pos], roll_ref.at[l, q, core, k], fin_s.at[c], fin_r.at[c], fsdp=partner
-            )
+            block = held_rows(c, pos)
+            push(block, block, fin_s.at[c], fin_r.at[c], fsdp=partner)
 
     def forward(j, c):
-        doubling[c, j].wait_recv()
+        await_blocks(c, 1 << j, ag_r.at[c, j])
         if j + 1 < bits:
             double(c, j + 1)
-        if j == 0:
-            finish(c, 0, 1)
         finish(c, 1 << j, 1 << j)
 
     stages = [gather_sum]
     stages += [functools.partial(add, i) for i in range(bits - 1)]
-    stages += [update, select]
+    stages += [update]
+    stages += [functools.partial(met, b) for b in range(tp_bits - 1)]
+    stages += [select]
     stages += [functools.partial(forward, j) for j in range(bits)]
     groups = [tuple(range(c, min(c + 2, chunks))) for c in range(0, chunks, 2)]
     for t in range(len(groups) + len(stages) - 1):
@@ -310,13 +338,24 @@
         raws[c].wait_send()
         for i in range(bits):
             halving[c, i].wait_send()
-            doubling[c, i].wait_send()
-        for d in range(1, tp):
-            spread[c, d].wait_send()
-        for sem in (out_s, fin_s, fin_r):
-            pltpu.make_async_copy(ag.at[c], ag.at[c], sem.at[c]).wait()
-    for wait in ends:
-        wait()
+            await_blocks(c, 1 << i, ag_s.at[c, i])
+        for b in range(tp_bits):
+            spread[c, b].wait_send()
+        for sem in (fin_s, fin_r):
+            await_blocks(c, pairs, sem.at[c])
+
+
+def write_out(*refs):
+    count = len(refs) // 2
+    copies = []
+    for i in range(count):
+        for l in range(refs[i].shape[0]):
+            sem = refs[-1].at[i, l]
+            copies.append(pltpu.make_async_copy(refs[i].at[l], refs[count + i].at[l], sem))
+    for copy in copies:
+        copy.start()
+    for copy in copies:
+        copy.wait()
 
 
 def fused(fsdp, tp, partials, token_counts, owner_map, params, moment1, moment2):
@@ -324,6 +363,7 @@
     per = params.shape[1]
     pairs = fsdp // 2
     bits = pairs.bit_length() - 1
+    tp_bits = tp.bit_length() - 1
     parts = next(n for n in range(SPLIT, 0, -1) if per % (n * TILE) == 0)
     rows = per // parts
     chunks = layers * parts
@@ -335,10 +375,10 @@
     outs = pl.pallas_call(
         functools.partial(kernel, (layers, fsdp, tp, parts, rows)),
         out_shape=[
-            jax.ShapeDtypeStruct(state, f32),
-            jax.ShapeDtypeStruct(state, f32),
-            jax.ShapeDtypeStruct(state, f32),
-            jax.ShapeDtypeStruct((layers, pairs, 2, parts, rows, width), b16),
+            pltpu.VMEM(state, f32),
+            pltpu.VMEM(state, f32),
+            pltpu.VMEM(state, f32),
+            pltpu.VMEM((layers, pairs, 2, parts, rows, width), b16),
         ],
         in_specs=[
             pl.BlockSpec(memory_space=pltpu.SMEM),
@@ -348,19 +388,15 @@
             anywhere,
             anywhere,
         ],
-        out_specs=[anywhere] * 4,
+        out_specs=[pl.BlockSpec(memory_space=pltpu.VMEM)] * 4,
         scratch_shapes=[
             pltpu.VMEM((fsdp, 8, width), f32),
             pltpu.VMEM((chunks, pairs, rows, width), b16),
             pltpu.VMEM((chunks, pairs, rows, width), b16),
             pltpu.VMEM((chunks, pairs, rows, width), f32),
             pltpu.VMEM((chunks, pairs, rows, width), f32),
-            pltpu.VMEM(state, f32),
-            pltpu.VMEM(state, f32),
-            pltpu.VMEM(state, f32),
-            pltpu.VMEM((chunks, rows, width), b16),
-            pltpu.VMEM((chunks, tp - 1, rows, width), b16),
-            pltpu.VMEM((chunks, pairs, rows, width), b16),
+            pltpu.VMEM((chunks, tp // 2, rows, width), b16),
+            pltpu.VMEM((chunks, 2, rows, width), b16),
             dma((fsdp,)),
             dma((fsdp,)),
             dma((3,)),
@@ -369,17 +405,15 @@
             dma((chunks,)),
             dma((chunks, bits)),
             dma((chunks, bits)),
-            dma((chunks, tp - 1)),
-            dma((chunks, tp - 1)),
+            dma((chunks, tp_bits)),
+            dma((chunks, tp_bits)),
             dma((chunks, bits)),
             dma((chunks, bits)),
             dma((chunks,)),
             dma((chunks,)),
-            dma((chunks,)),
-            dma((chunks, 3)),
         ],
         compiler_params=pltpu.CompilerParams(
-            collective_id=0, has_side_effects=True, vmem_limit_bytes=56 * 1024 * 1024
+            collective_id=0, has_side_effects=True, vmem_limit_bytes=48 * 1024 * 1024
         ),
     )(
         owner_map,
@@ -389,13 +423,23 @@
         moment1.reshape(state),
         moment2.reshape(state),
     )
-    return (*(out.reshape(params.shape) for out in outs[:3]), outs[3].reshape(layers, depth, width))
+    outs = [out.reshape(params.shape) for out in outs[:3]] + [outs[3].reshape(layers, depth, width)]
+    return tuple(
+        pl.pallas_call(
+            write_out,
+            out_shape=[jax.ShapeDtypeStruct(out.shape, out.dtype) for out in outs],
+            in_specs=[pl.BlockSpec(memory_space=pltpu.VMEM)] * 4,
+            out_specs=[anywhere] * 4,
+            scratch_shapes=[dma((4, layers))],
+            compiler_params=pltpu.CompilerParams(vmem_limit_bytes=16 * 1024 * 1024),
+        )(*outs)
+    )
 
 
 def solution(mesh):
     fsdp, tp = mesh.shape["fsdp"], mesh.shape["tp"]
     local = plain
-    if fsdp >= 4 and fsdp & (fsdp - 1) == 0 and tp > 1:
+    if fsdp >= 4 and fsdp & (fsdp - 1) == 0 and tp > 1 and tp & (tp - 1) == 0:
         local = functools.partial(fused, fsdp, tp)
     in_specs = (
         P("fsdp", None, None, "tp"),

time: 111 us -> 93.4 us (0.84)
  local copies, waits for them, and re-layouts: 10.5 us -> 0.6 us
  Pallas kernels: 99.5 us -> 91.3 us
    pallas_call x1, Pallas kernels: 99.5 us -> 87.5 us  [fused(): pl.pallas_call(functools.partial(kernel, (layers, fsdp, tp, parts, rows))...]
    unnamed x6 -> x0, local copies, waits for them, and re-layouts: 9.88 us -> none
    pallas_call x0 -> x1, Pallas kernels: none -> 3.72 us  [fused(): pl.pallas_call(write_out, out_shape=[jax.ShapeDtypeStruct(out.shape, out....]
where the time goes in v2:
time: 93.4 us; the launch traced here: 93.1 us
  Pallas kernels  91.3 us (98%)
  between operations  1.29 us (1%)
    pallas_call x1, Pallas kernels, fused(): pl.pallas_call(functools.partial(kernel, (layers, fsdp, tp, parts, rows))...  87.5 us
    pallas_call x1, Pallas kernels, fused(): pl.pallas_call(write_out, out_shape=[jax.ShapeDtypeStruct(out.shape, out....  3.72 us

profile of v2, /device:TPU:0, one launch (start us, length us, event | category | flops | bytes accessed | tf_op | source)
XLA Modules:
  0.0 93.1 jit_solution(4996498111482641082)
XLA Ops:
  1.3 0.6 broadcast_in_dim.9.w_ref
  1.9 87.5 %shard_map.93 = (f32[2,4,160,256]{3,2,1,0:T(8,128)S(1)}, f32[2,4,160,256]{3,2,1,0:T(8,128)S(1)}, f32[2,4,160,256]{3,2,1,0:T(8,128)S(1)}, bf16[2,4,2,4,160,256]{5,4,3,2,1,0:T(8,128)(2,1)S(1)}) custom-call(s32[2,4]{1,0:T(2,128)} %owner_ref.1, f32[8,256]{1,0:T(8,128)} %broadcast_in_dim.9.w_ref, bf16[2,4,2,4,160,256]{5,4,3,2,1,0:T(8,128)(2,1)} %bitcast.13, ...), custom_call_target="tpu_custom_call" | custom-call | tf_op jit(solution)/shard_map/pallas_call | solution.py:375
  89.4 3.7 %shard_map.94 = (f32[2,640,256]{2,1,0:T(8,128)}, f32[2,640,256]{2,1,0:T(8,128)}, f32[2,640,256]{2,1,0:T(8,128)}, bf16[2,5120,256]{2,1,0:T(8,128)(2,1)}) custom-call(f32[2,640,256]{2,1,0:T(8,128)S(1)} %bitcast.10, f32[2,640,256]{2,1,0:T(8,128)S(1)} %bitcast.11, f32[2,640,256]{2,1,0:T(8,128)S(1)} %bitcast.12, bf16[2,5120,256]{2,1,0:T(8,128)(2,1)S(1)} %bitcast.9), custom_call_target="tpu_custom_call" | custom-call | tf_op jit(solution)/shard_map/pallas_call | solution.py:428

commit v3 on v2

--- a/solution.py
+++ b/solution.py
@@ -9,8 +9,9 @@
 
 STEP = 10
 MESH = pl.DeviceIdType.MESH
-SPLIT = 4
+SPLIT = 8
 TILE = 16
+SPAN = 80
 
 
 def plain(partials, token_counts, owner_map, params, moment1, moment2):
@@ -112,12 +113,6 @@
         load = pltpu.make_async_copy(part_ref.at[l, :, core, k], mine.at[c], ld_s.at[c])
         load.start()
         loads.append(load)
-    opts = []
-    for i, (src, dst) in enumerate(((p_ref, np_ref), (m_ref, nm_ref), (v_ref, nv_ref))):
-        load = pltpu.make_async_copy(src, dst, opt_s.at[i])
-        load.start()
-        opts.append(load)
-
     pl.semaphore_wait(barrier, fsdp - 1 + tp_bits)
 
     def push(src, dst, send, arrive, **device):
@@ -132,11 +127,7 @@
         copy.start()
         return copy
 
-    weights = []
-    for d in range(1, fsdp):
-        weights.append(
-            push(w_ref, wbuf.at[d], w_s.at[d], w_r.at[d], fsdp=lax.rem(me + d, fsdp))
-        )
+    weights = [push(w_ref, wbuf.at[0], w_s.at[0], w_r.at[0], fsdp=partner)]
     raws = []
     for c in range(chunks):
         l, k = where(c)
@@ -149,14 +140,28 @@
                 fsdp=partner,
             )
         )
-    for copy in weights:
-        copy.wait()
+    for d in range(1, fsdp):
+        weights.append(
+            push(w_ref, wbuf.at[d], w_s.at[d], w_r.at[d], fsdp=lax.rem(me + d, fsdp))
+        )
+    opts = []
+    for i, (src, dst) in enumerate(((p_ref, np_ref), (m_ref, nm_ref), (v_ref, nv_ref))):
+        load = pltpu.make_async_copy(src, dst, opt_s.at[i])
+        load.start()
+        opts.append(load)
+
     my_weight = w_ref[0:1, :]
-    total = my_weight
-    for d in range(1, fsdp):
-        total = total + wbuf[d, 0:1, :]
-    other_weight = jnp.where(core == 1, wbuf[1, 0:1, :], wbuf[fsdp - 1, 0:1, :])
-    scale = 1.0 / total
+    weights[0].wait()
+    other_weight = wbuf[0, 0:1, :]
+
+    def weigh():
+        total = my_weight
+        for d in range(1, fsdp):
+            weights[d].wait()
+            total = total + wbuf[d, 0:1, :]
+        return 1.0 / total
+
+    scale = []
 
     def order(c):
         names = list(range(bits))
@@ -165,7 +170,7 @@
     def flipped(flips):
         return away(mine_q, flips)
 
-    step = 2 * TILE if rows % (2 * TILE) == 0 else TILE
+    step = next(n for n in range(min(rows, SPAN), 0, -TILE) if rows % n == 0)
 
     def tiles(body):
         def run(i, carry):
@@ -237,9 +242,10 @@
         if c == 0:
             for load in opts:
                 load.wait()
+            scale.append(weigh())
 
         def body(at):
-            grad = (acc[c, 0, at, :] + recv[c, 1, at, :]) * scale
+            grad = (acc[c, 0, at, :] + recv[c, 1, at, :]) * scale[0]
             first, second, direction, new_params = adam(
                 grad, np_ref[l, k, at, :], nm_ref[l, k, at, :], nv_ref[l, k, at, :]
             )

time: 93.4 us -> 86.1 us (0.922)
  Pallas kernels: 91.3 us -> 84 us
    pallas_call x1, Pallas kernels: 87.5 us -> 80.3 us  [fused(): pl.pallas_call(functools.partial(kernel, (layers, fsdp, tp, parts, rows))...]
where the time goes in v3:
time: 86.1 us; the launch traced here: 85.9 us
  Pallas kernels  84 us (98%)
  between operations  1.29 us (1%)
    pallas_call x1, Pallas kernels, fused(): pl.pallas_call(functools.partial(kernel, (layers, fsdp, tp, parts, rows))...  80.3 us
    pallas_call x1, Pallas kernels, fused(): pl.pallas_call(write_out, out_shape=[jax.ShapeDtypeStruct(out.shape, out....  3.72 us

profile of v3, /device:TPU:0, one launch (start us, length us, event | category | flops | bytes accessed | tf_op | source)
XLA Modules:
  0.0 85.9 jit_solution(3483593486297903058)
XLA Ops:
  1.3 0.6 broadcast_in_dim.9.w_ref
  1.9 80.3 %shard_map.93 = (f32[2,8,80,256]{3,2,1,0:T(8,128)S(1)}, f32[2,8,80,256]{3,2,1,0:T(8,128)S(1)}, f32[2,8,80,256]{3,2,1,0:T(8,128)S(1)}, bf16[2,4,2,8,80,256]{5,4,3,2,1,0:T(8,128)(2,1)S(1)}) custom-call(s32[2,4]{1,0:T(2,128)} %owner_ref.1, f32[8,256]{1,0:T(8,128)} %broadcast_in_dim.9.w_ref, bf16[2,4,2,8,80,256]{5,4,3,2,1,0:T(8,128)(2,1)} %bitcast.13, ...), custom_call_target="tpu_custom_call" | custom-call | tf_op jit(solution)/shard_map/pallas_call | solution.py:381
  82.1 3.7 %shard_map.94 = (f32[2,640,256]{2,1,0:T(8,128)}, f32[2,640,256]{2,1,0:T(8,128)}, f32[2,640,256]{2,1,0:T(8,128)}, bf16[2,5120,256]{2,1,0:T(8,128)(2,1)}) custom-call(f32[2,640,256]{2,1,0:T(8,128)S(1)} %bitcast.10, f32[2,640,256]{2,1,0:T(8,128)S(1)} %bitcast.11, f32[2,640,256]{2,1,0:T(8,128)S(1)} %bitcast.12, bf16[2,5120,256]{2,1,0:T(8,128)(2,1)S(1)} %bitcast.9), custom_call_target="tpu_custom_call" | custom-call | tf_op jit(solution)/shard_map/pallas_call | solution.py:434
